TPU v7x, 32 devices: a whole 2x2x4 slice. The times are simulated.
32 devices in a mesh: blk: 4 (over y, x), grp: 8 (over z, core).
Axes of the slice: x: 2, y: 2, z: 4, core: 2. Of those that a mesh axis runs over, the one named last changes fastest.
Arguments:
- points: float32 [3, 4096], P(None, ('blk', 'grp')), may hold values from 0 to 1
- labels: int32 [4096], P(('blk', 'grp')), may hold values 0 or 1
- shape_scale: float32 [4096], P(('blk', 'grp')), may hold values from 0.1 to 0.4
- krylov_basis: float32 [8, 32, 4096], P(None, None, ('blk', 'grp')), may hold values from -6 to 6
- sketch: float32 [1024, 4096], P(None, ('blk', 'grp')), may hold values from -0.09375 to 0.09375
- sketched_basis: float32 [8, 32, 1024], replicated, may hold values from -0.1875 to 0.1875
Outputs:
- next_vector: float32 [32, 4096], P(None, ('blk', 'grp'))
- coefficients: float32 [8, 32], replicated
- sketch_next: float32 [32, 1024], replicated
- norms: float32 [32], replicated
All inputs are finite; a program needn't handle non-finite values. No bound on the sum of `labels` on one device may be relied on, other than what follows from the above.
Results may differ from a plain program's by a relative error of at most 0.0003.
Values sent between devices are 32-bit elements; how exact they have to be, the bound alone decides.
A program may use at most 64 MiB of HBM per device.

v0:
```python
import math
import jax
import jax.numpy as jnp
from jax import lax
from jax.sharding import PartitionSpec as P

SYSTEMS = 32
KRYLOV = 8


def kernel_terms(target_points, target_labels, source_block):
    source_points = source_block[0:3]
    scales = source_block[3]
    weights_block = source_block[4:]
    delta_x = source_points[0][:, None] - target_points[0][None, :]
    delta_y = source_points[1][:, None] - target_points[1][None, :]
    delta_z = source_points[2][:, None] - target_points[2][None, :]
    radius_sq = delta_x * delta_x + delta_y * delta_y + delta_z * delta_z
    squared_scale = (scales * scales)[:, None]
    shifted = radius_sq + squared_scale
    inverse = lax.rsqrt(shifted)
    boundary = shifted * inverse
    interior = (3.0 * squared_scale + 2.0 * radius_sq) * inverse * inverse * inverse
    kernel = jnp.where(target_labels[None, :] == 1, interior, boundary)
    return jnp.dot(
        weights_block, kernel, precision=lax.Precision.HIGHEST, preferred_element_type=jnp.float32
    )


def block_size(length, wanted):
    return wanted if length % wanted == 0 else length


def accumulate(running, target_points, target_labels, source_block):
    target_count = target_points.shape[1]
    source_count = source_block.shape[1]
    tblock = block_size(target_count, 2048)
    sblock = block_size(source_count, 2048)
    system_rows = running.shape[0]

    def over_targets(target_index, current):

        def over_sources(source_index, partial_value):
            portion = lax.dynamic_slice_in_dim(source_block, source_index * sblock, sblock, 1)
            return partial_value + kernel_terms(target_points, target_labels, portion)

        partial_value = lax.fori_loop(
            0, source_count // sblock, over_sources, jnp.zeros((system_rows, tblock), jnp.float32)
        )
        return current + partial_value

    return lax.fori_loop(0, target_count // tblock, over_targets, running)


def shards(points, labels, shape_scale, krylov_basis, sketch, sketched_basis):
    own_count = points.shape[1]
    everything = lax.axis_size("blk") * lax.axis_size("grp") * own_count
    sources = jnp.concatenate([points, shape_scale[None, :], krylov_basis[KRYLOV - 1]], axis=0)
    empty = jnp.zeros((SYSTEMS, own_count), jnp.float32)
    summed = accumulate(
        empty, points, labels, lax.all_gather(sources, ("blk", "grp"), axis=1, tiled=True)
    )
    image = summed / math.sqrt(everything)
    local_sketch = lax.dot_general(
        image,
        sketch,
        (((1,), (1,)), ((), ())),
        precision=lax.Precision.HIGHEST,
        preferred_element_type=jnp.float32,
    )
    sketched = lax.psum(local_sketch, ("blk", "grp"))
    coefficients = jnp.einsum(
        "jrk,rk->jr", sketched_basis, sketched, precision=lax.Precision.HIGHEST
    )
    remainder = sketched - jnp.einsum(
        "jr,jrk->rk", coefficients, sketched_basis, precision=lax.Precision.HIGHEST
    )
    norms = jnp.sqrt(jnp.mean(remainder * remainder, axis=1) + 1e-06)
    sketch_next = remainder / norms[:, None]
    reduced = image - jnp.einsum(
        "jr,jrn->rn", coefficients, krylov_basis, precision=lax.Precision.HIGHEST
    )
    next_vector = reduced / norms[:, None]
    return (next_vector, coefficients, sketch_next, norms)


def solution(mesh):
    placed = (
        P(None, ("blk", "grp")),
        P(("blk", "grp")),
        P(("blk", "grp")),
        P(None, None, ("blk", "grp")),
        P(None, ("blk", "grp")),
        P(),
    )
    return jax.shard_map(
        shards,
        mesh=mesh,
        in_specs=placed,
        out_specs=(P(None, ("blk", "grp")), P(), P(), P()),
        check_vma=False,
    )
```

profile of v0, /device:TPU:0, one launch (start us, length us, event | category | flops | bytes accessed | tf_op | source)
XLA Modules:
  0.0 195.9 jit_solution(17373773227067051160)
XLA Ops:
  7.2 0.0 copy-start
  7.2 0.0 all-reduce.2.cloned.1.call-start
  7.2 0.0 copy-start.4
  7.2 0.8 slice_bitcast_fusion.3
  8.0 0.0 copy-start.7
  8.1 0.0 copy-done.4
  8.1 0.7 copy-done.7
  8.7 0.0 copy-start.8
  8.7 45.9 %all_gather.3 = f32[36,4096]{1,0:T(8,128)S(1)} all-gather(f32[36,128]{1,0:T(8,128)S(1)} %pad_maximum_fusion), channel_id=1, replica_groups=mesh['blk'=4,'grp'=8] {'blk','grp'}, dimensions={1}, use_global_device_ids=true | all-gather | bytes 608256 | tf_op jit(solution)/shard_map/all_gather | solution.py:61
  54.7 0.0 copy-done.8
  54.7 0.0 copy-start.2
  54.7 4.4 %while.21 = (s32[]{:T(128)}, f32[32,128]{1,0:T(8,128)S(1)}, f32[36,4096]{1,0:T(8,128)S(1)}, s32[128]{0:T(128)S(1)}, f32[3,128]{1,0:T(4,128)S(1)}, /*index=5*/s32...) while((s32[]{:T(128)}, f32[32,128]{1,0:T(8,128)S(1)}, ...), condition=%wide.region_1.0_spmd.clone, body=%wide.region_0.1_spmd.clone.sunk | while | flops 104870024 | bytes 423813 | solution.py:47
  54.7 0.1 constant_dynamic-slice_fusion.2
  54.8 2.0 %convolution_add_fusion.2 = f32[32,128]{1,0:T(8,128)S(1)} fusion(f32[2048]{0:T(1024)S(1)} %bitcast.42, f32[128]{0:T(128)S(1)} %get-tuple-element.195, f32[2048]{0:T(1024)S(1)} %bitcast.45, f32[128]{0:T(128)S(1)} %get-tuple-element.197, f32[2048]{0:T(1024)S(1)} %bitcast.44, f32[128]{0:T(128)S(1)} %get-tuple-element.199, f32[2048]{0:T(1024)S(1)} %bitcast.43, ...), kind=kOutput, calls=%fused_computation.2.clone.1 | convolution fusion | flops 104865792 | bytes 337929 | tf_op jit(solution)/shard_map/while/body/eval_jaxpr/while/body/eval_jaxpr/dot_general | solution.py:25
  56.9 0.1 constant_dynamic-slice_fusion.2
  57.0 2.0 %convolution_add_fusion.2 = f32[32,128]{1,0:T(8,128)S(1)} fusion(f32[2048]{0:T(1024)S(1)} %bitcast.42, f32[128]{0:T(128)S(1)} %get-tuple-element.195, f32[2048]{0:T(1024)S(1)} %bitcast.45, f32[128]{0:T(128)S(1)} %get-tuple-element.197, f32[2048]{0:T(1024)S(1)} %bitcast.44, f32[128]{0:T(128)S(1)} %get-tuple-element.199, f32[2048]{0:T(1024)S(1)} %bitcast.43, ...), kind=kOutput, calls=%fused_computation.2.clone.1 | convolution fusion | flops 104865792 | bytes 337929 | tf_op jit(solution)/shard_map/while/body/eval_jaxpr/while/body/eval_jaxpr/dot_general | solution.py:25
  59.1 0.0 copy-done.2
  59.1 1.3 fusion.32
  60.3 0.0 all-reduce.2.cloned.1.call-update
  60.4 120.9 %all-reduce.2.cloned.1.call-done = f32[32,1024]{1,0:T(8,128)} async-done(((f32[32,1024]{1,0:T(8,128)}), f32[32,1024]{1,0:T(8,128)}) %all-reduce.2.cloned.1.call-update) | async-done | bytes 131088 | tf_op jit(solution)/shard_map/psum | solution.py:71
  181.2 0.0 copy-done
  181.2 0.0 copy-start.3
  181.3 3.6 %fusion.27 = f32[32,1,8]{2,1,0:T(1,128)S(1)} fusion(f32[8,32,1024]{2,1,0:T(8,128)S(1)} %copy-done, f32[32,1024,1]{1,0,2:T(8,128)} %bitcast.40), kind=kOutput, calls=%fused_computation.36 | convolution fusion | flops 3145728 | bytes 1180672 | tf_op jit(solution)/shard_map/jrk,rk->jr/dot_general | solution.py:72
  184.8 0.1 copy.12
  184.9 0.0 copy-start.5
  184.9 0.1 copy.13
  185.0 0.5 copy-done.5
  185.5 0.0 copy-done.3
  185.5 0.4 fusion.29
  185.9 0.0 copy-start.1
  185.9 1.5 fusion.25
  187.4 0.0 copy-done.1
  187.4 0.1 multiply_reduce_fusion
  187.6 0.0 copy-start.6
  187.6 0.7 subtract_divide_fusion
  188.3 0.0 copy-done.6
  188.3 0.7 broadcast_divide_fusion
  (9 shorter events, 0.0 us)
Async XLA Ops:
  7.2 174.1 %copy-start = (f32[8,32,1024]{2,1,0:T(8,128)S(1)}, f32[8,32,1024]{2,1,0:T(8,128)}, u32[]{:S(2)}) copy-start(f32[8,32,1024]{2,1,0:T(8,128)} %param.13) | copy-start | bytes 3145732
  7.2 174.1 %all-reduce.2.cloned.1.call-start = ((), (), s32[]{:S(2)}) async-start(), calls=%async_computation | async-start | bytes 262144 | tf_op jit(solution)/shard_map/psum | solution.py:71
  7.2 0.8 copy-start.4
  8.0 0.7 copy-start.7
  8.7 46.0 %copy-start.8 = (s32[128]{0:T(128)S(1)}, s32[128]{0:T(128)}, u32[]{:S(2)}) copy-start(s32[128]{0:T(128)} %param.9) | copy-start | bytes 1540
  54.7 4.4 %copy-start.2 = (f32[1024,128]{1,0:T(8,128)S(1)}, f32[1024,128]{1,0:T(8,128)}, u32[]{:S(2)}) copy-start(f32[1024,128]{1,0:T(8,128)} %param.12) | copy-start | bytes 1572868
  181.2 4.3 %copy-start.3 = (f32[8,32,128]{2,1,0:T(8,128)S(1)}, f32[8,32,128]{2,1,0:T(8,128)}, u32[]{:S(2)}) copy-start(f32[8,32,128]{2,1,0:T(8,128)} %param.11) | copy-start | bytes 393220
  184.9 0.6 copy-start.5
  185.9 1.5 copy-start.1
  187.6 0.7 copy-start.6
Sparse Core Ops, SparseCore 0:
  60.5 120.7 all-reduce.1
where the time goes:
time: 196 us
  waiting for transfers between devices  121 us (62%)
  blocking collectives  45.9 us (23%)
  between operations  14.1 us (7%)
  matrix products  10.7 us (5%)
  local copies, waits for them, and re-layouts  2.17 us (1%)
    psum x1, waiting for transfers between devices, shards(): sketched = lax.psum(local_sketch, ('blk', 'grp'))  121 us
    all_gather x1, blocking collectives, shards(): lax.all_gather(sources, ('blk', 'grp'), axis=1, tiled=True)  45.9 us
    dot_general x2, matrix products, kernel_terms(): jnp.dot(weights_block, kernel, precision=lax.Precision.HIGHEST, preferred...  4 us
  transfers between devices with their start and end apart: 1, of which 1 were waited for; matrix products, arithmetic and copies ran while one was open for 0% of the time, Pallas kernels for 0%

commit v1 on v0

--- a/solution.py
+++ b/solution.py
@@ -58,7 +58,7 @@
     sources = jnp.concatenate([points, shape_scale[None, :], krylov_basis[KRYLOV - 1]], axis=0)
     empty = jnp.zeros((SYSTEMS, own_count), jnp.float32)
     summed = accumulate(
-        empty, points, labels, lax.all_gather(sources, ("blk", "grp"), axis=1, tiled=True)
+        empty, points, labels, jnp.concatenate(lax.all_gather(sources, ("blk", "grp")), axis=1)
     )
     image = summed / math.sqrt(everything)
     local_sketch = lax.dot_general(

time: 196 us -> 198 us (1.010)
  no operation moved by 1% of the time
where the time goes in v1:
time: 198 us
  waiting for transfers between devices  121 us (61%)
  blocking collectives  45.9 us (23%)
  between operations  14.1 us (7%)
  matrix products  10.7 us (5%)
  local copies, waits for them, and re-layouts  3.84 us (2%)
    psum x1, waiting for transfers between devices, shards(): sketched = lax.psum(local_sketch, ('blk', 'grp'))  121 us
    all_gather x1, blocking collectives, shards(): lax.all_gather(sources, ('blk', 'grp'))  45.9 us
    dot_general x2, matrix products, kernel_terms(): jnp.dot(weights_block, kernel, precision=lax.Precision.HIGHEST, preferred...  3.99 us
  transfers between devices with their start and end apart: 1, of which 1 were waited for; matrix products, arithmetic and copies ran while one was open for 0% of the time, Pallas kernels for 0%

profile of v1, /device:TPU:0, one launch (start us, length us, event | category | flops | bytes accessed | tf_op | source)
XLA Modules:
  0.0 197.5 jit_solution(17060423394985711732)
XLA Ops:
  7.2 0.0 copy-start
  7.2 0.0 all-reduce.2.cloned.1.call-start
  7.2 0.0 copy-start.4
  7.2 0.8 slice_bitcast_fusion.3
  8.0 0.0 copy-start.7
  8.1 0.0 copy-done.4
  8.1 0.7 copy-done.7
  8.7 45.9 %all-gather.1 = f32[32,36,128]{2,1,0:T(8,128)S(1)} all-gather(f32[1,36,128]{2,1,0:T(8,128)S(1)} %maximum_bitcast_fusion), channel_id=2, replica_groups=mesh['blk'=4,'grp'=8] {'blk','grp'}, dimensions={0}, use_global_device_ids=true | all-gather | bytes 608256 | tf_op jit(solution)/shard_map/all_gather | solution.py:61
  54.6 0.1 copy.11
  54.8 0.1 pad.3
  54.8 0.4 copy.19
  55.2 0.0 copy-start.8
  55.2 0.6 copy-done.8
  55.9 0.0 copy-start.2
  55.9 4.4 %while.21 = (s32[]{:T(128)}, f32[32,128]{1,0:T(8,128)S(1)}, f32[36,4096]{1,0:T(8,128)S(1)}, s32[128]{0:T(128)S(1)}, f32[3,128]{1,0:T(4,128)S(1)}, /*index=5*/s32...) while((s32[]{:T(128)}, f32[32,128]{1,0:T(8,128)S(1)}, ...), condition=%wide.region_1.0_spmd.clone, body=%wide.region_0.1_spmd.clone.sunk | while | flops 104870024 | bytes 423805 | solution.py:47
  55.9 0.1 constant_dynamic-slice_fusion.2
  56.0 2.0 %convolution_add_fusion.2 = f32[32,128]{1,0:T(8,128)S(1)} fusion(f32[2048]{0:T(1024)S(1)} %bitcast.51, f32[128]{0:T(128)S(1)} %get-tuple-element.195, f32[2048]{0:T(1024)S(1)} %bitcast.54, f32[128]{0:T(128)S(1)} %get-tuple-element.197, f32[2048]{0:T(1024)S(1)} %bitcast.53, f32[128]{0:T(128)S(1)} %get-tuple-element.199, f32[2048]{0:T(1024)S(1)} %bitcast.52, ...), kind=kOutput, calls=%fused_computation.2.clone.1 | convolution fusion | flops 104865792 | bytes 337929 | tf_op jit(solution)/shard_map/while/body/eval_jaxpr/while/body/eval_jaxpr/dot_general | solution.py:25
  58.1 0.1 constant_dynamic-slice_fusion.2
  58.2 2.0 %convolution_add_fusion.2 = f32[32,128]{1,0:T(8,128)S(1)} fusion(f32[2048]{0:T(1024)S(1)} %bitcast.51, f32[128]{0:T(128)S(1)} %get-tuple-element.195, f32[2048]{0:T(1024)S(1)} %bitcast.54, f32[128]{0:T(128)S(1)} %get-tuple-element.197, f32[2048]{0:T(1024)S(1)} %bitcast.53, f32[128]{0:T(128)S(1)} %get-tuple-element.199, f32[2048]{0:T(1024)S(1)} %bitcast.52, ...), kind=kOutput, calls=%fused_computation.2.clone.1 | convolution fusion | flops 104865792 | bytes 337929 | tf_op jit(solution)/shard_map/while/body/eval_jaxpr/while/body/eval_jaxpr/dot_general | solution.py:25
  60.3 0.0 copy-done.2
  60.3 1.3 fusion.32
  61.5 0.0 all-reduce.2.cloned.1.call-update
  61.6 120.9 %all-reduce.2.cloned.1.call-done = f32[32,1024]{1,0:T(8,128)} async-done(((f32[32,1024]{1,0:T(8,128)}), f32[32,1024]{1,0:T(8,128)}) %all-reduce.2.cloned.1.call-update) | async-done | bytes 131088 | tf_op jit(solution)/shard_map/psum | solution.py:71
  182.4 0.0 copy-done
  182.5 3.5 %fusion.27 = f32[32,1,8]{2,1,0:T(1,128)S(1)} fusion(f32[8,32,1024]{2,1,0:T(8,128)S(1)} %copy-done, f32[32,1024,1]{1,0,2:T(8,128)} %bitcast.48), kind=kOutput, calls=%fused_computation.36 | convolution fusion | flops 3145728 | bytes 1180672 | tf_op jit(solution)/shard_map/jrk,rk->jr/dot_general | solution.py:72
  186.0 0.1 copy.14
  186.1 0.0 copy-start.5
  186.1 0.1 copy.15
  186.1 0.5 copy-done.5
  186.7 0.0 copy-start.3
  186.7 1.5 fusion.25
  188.2 0.0 copy-done.3
  188.2 0.0 copy-start.1
  188.2 0.4 fusion.29
  188.6 0.5 copy-done.1
  189.1 0.1 multiply_reduce_fusion
  189.2 0.0 copy-start.6
  189.2 0.7 subtract_divide_fusion
  189.9 0.0 copy-done.6
  189.9 0.7 broadcast_divide_fusion
  (9 shorter events, 0.0 us)
Async XLA Ops:
  7.2 175.3 %copy-start = (f32[8,32,1024]{2,1,0:T(8,128)S(1)}, f32[8,32,1024]{2,1,0:T(8,128)}, u32[]{:S(2)}) copy-start(f32[8,32,1024]{2,1,0:T(8,128)} %param.13) | copy-start | bytes 3145732
  7.2 175.3 %all-reduce.2.cloned.1.call-start = ((), (), s32[]{:S(2)}) async-start(), calls=%async_computation | async-start | bytes 262144 | tf_op jit(solution)/shard_map/psum | solution.py:71
  7.2 0.8 copy-start.4
  8.0 0.7 copy-start.7
  55.2 0.7 copy-start.8
  55.9 4.4 %copy-start.2 = (f32[1024,128]{1,0:T(8,128)S(1)}, f32[1024,128]{1,0:T(8,128)}, u32[]{:S(2)}) copy-start(f32[1024,128]{1,0:T(8,128)} %param.12) | copy-start | bytes 1572868
  186.1 0.6 copy-start.5
  186.7 1.5 copy-start.3
  188.2 0.9 copy-start.1
  189.2 0.7 copy-start.6
Sparse Core Ops, SparseCore 0:
  61.7 120.7 all-reduce.1
